TPU v7x, 32 devices: a whole 2x2x4 slice. The times are simulated.
32 devices in a mesh: rows: 8 (over z, y), cols: 4 (over x, core).
Axes of the slice: x: 2, y: 2, z: 4, core: 2. Of those that a mesh axis runs over, the one named last changes fastest.
Arguments:
- panel: float32 [16384, 256], P(('rows', 'cols')), may hold values from -17 to 17, as said below
- trailing: float32 [16384, 2048], P('rows', 'cols'), may hold values from -6 to 6
Outputs:
- rfactor: float32 [256, 256], replicated
- projected: float32 [256, 2048], P(None, 'cols')
- updated: float32 [16384, 2048], P('rows', 'cols')
Inputs may be any that keep to these rules, and one draw needn't show every extreme that they name: The panel has full column rank with a moderate condition number (under 100); each column has its own scale and a part shared by all columns.
All inputs are finite; a program needn't handle non-finite values.
Results may differ from a plain program's by a relative error of at most 0.000078.
Values sent between devices are 32-bit elements; how exact they have to be, the bound alone decides.
A program may use at most 64 MiB of HBM per device.

v0:
```python
import jax
import jax.numpy as jnp
from jax import lax
from jax.sharding import PartitionSpec as P


def inner(left, right):
    return lax.dot_general(
        left,
        right,
        (((0,), (0,)), ((), ())),
        precision=lax.Precision.HIGHEST,
        preferred_element_type=jnp.float32,
    )


def times(left, right):
    return jnp.dot(left, right, precision=lax.Precision.HIGHEST, preferred_element_type=jnp.float32)


def lower_solve(rfactor, right):
    return jax.scipy.linalg.solve_triangular(rfactor.T, right, lower=True)


def shards(panel, trailing):
    block = lax.all_gather(panel, "cols", axis=0, tiled=True)
    gram, cross = lax.psum((inner(block, block), inner(block, trailing)), "rows")
    rfactor = jnp.linalg.cholesky(gram).T
    basis = lower_solve(rfactor, block.T).T
    projected = lower_solve(rfactor, cross)
    updated = trailing - times(basis, projected)
    return (rfactor, projected, updated)


def solution(mesh):
    placed = (P(("rows", "cols"), None), P("rows", "cols"))
    return jax.shard_map(
        shards,
        mesh=mesh,
        in_specs=placed,
        out_specs=(P(), P(None, "cols"), P("rows", "cols")),
        check_vma=False,
    )
```

profile of v0, /device:TPU:0, one launch (start us, length us, event | category | flops | bytes accessed | tf_op | source)
XLA Modules:
  0.0 203.5 jit_solution(6136574785826408481)
XLA Ops:
  7.2 0.0 all-gather.2.cloned.1.call-start
  7.2 0.7 all-gather.2.cloned.1.call-update
  7.9 0.0 all-reduce.4.cloned.1.call-start
  7.9 26.9 %all-gather.2.cloned.1.call-done = f32[2048,256]{1,0:T(8,128)} async-done(((f32[512,256]{1,0:T(8,128)}), f32[2048,256]{1,0:T(8,128)}) %all-gather.2.cloned.1.call-update) | async-done | bytes 2097168 | tf_op jit(solution)/shard_map/all_gather | solution.py:26
  34.8 0.0 copy-start
  34.9 6.5 %fusion.19 = f32[256,256]{0,1:T(8,128)} fusion(f32[2048,256]{1,0:T(8,128)} %all-gather.2.cloned.1.call-done), kind=kOutput, calls=%fused_computation.41 | convolution fusion | flops 1610612736 | bytes 2359296 | tf_op jit(solution)/shard_map/dot_general | solution.py:8
  41.4 0.0 copy-done
  41.4 6.6 %fusion.20 = f32[256,512]{1,0:T(8,128)} fusion(f32[2048,256]{1,0:T(8,128)S(1)} %copy-done, f32[2048,512]{1,0:T(8,128)} %param.3), kind=kOutput, calls=%fused_computation.42 | convolution fusion | flops 3221225472 | bytes 6815744 | tf_op jit(solution)/shard_map/dot_general | solution.py:8
  48.0 0.0 all-reduce.4.cloned.1.call-update
  48.1 75.3 %all-reduce.4.cloned.1.call-done = (f32[256,256]{0,1:T(8,128)}, f32[256,512]{1,0:T(8,128)}) async-done(((f32[256,256]{0,1:T(8,128)}, f32[256,512]{1,0:T(8,128)}), (f32[256,256]{0,1:T(8,128)}, f32[256,512]{1,0:T(8,128)})) %all-reduce.4.cloned.1.call-update) | async-done | bytes 786448 | tf_op jit(solution)/shard_map/psum | solution.py:27
  123.4 1.1 copy.6
  124.5 0.0 copy-start.3
  124.5 1.0 fusion.7
  125.6 11.7 %cholesky.50 = f32[128,128]{1,0:T(8,128)S(1)} custom-call(f32[128,128]{1,0:T(8,128)S(1)} %cholesky.118), custom_call_target="Cholesky" | custom-call | tf_op jit(solution)/shard_map/jit(cholesky)/cholesky | solution.py:28
  137.3 9.9 %custom-call.18 = f32[1,128,128]{1,2,0:T(8,128)S(1)} custom-call(f32[1,128,128]{2,1,0:T(8,128)S(1)} %get-tuple-element.31), custom_call_target="InvertDiagBlocksLowerTriangular" | custom-call | tf_op jit(solution)/shard_map/jit(cholesky)/cholesky | solution.py:28
  147.3 0.2 constant_dynamic-update-slice_fusion.1
  147.5 0.3 convolution_subtract_fusion.3
  147.8 11.7 %cholesky.105 = f32[128,128]{1,0:T(8,128)S(1)} custom-call(f32[128,128]{1,0:T(8,128)S(1)} %convolution_subtract_fusion.3), custom_call_target="Cholesky" | custom-call | tf_op jit(solution)/shard_map/jit(cholesky)/cholesky | solution.py:28
  159.5 0.6 compare_reduce_fusion
  161.5 0.8 copy.7
  162.3 0.1 triangular_solve.57
  162.4 4.0 %while.1 = (s32[]{:T(128)}, f32[256,256]{1,0:T(8,128)S(1)}, s32[2,2]{1,0:T(2,128)S(1)}, f32[2,128,128]{2,1,0:T(8,128)S(1)}, s32[]{:T(128)}) while((s32[]{:T(128)}, f32[256,256]{1,0:T(8,128)S(1)}, s32[2,2]{1,0:T(2,128)S(1)}, f32[2,128,128]{2,1,0:T(8,128)S(1)}, s32[]{:T(128)}) %tuple.29), condition=%wide.while_cond, body=%wide.while_body.sunk | while | flops 2 | bytes 131189 | solution.py:22
  162.4 0.6 fusion.33
  163.0 1.4 bitcast_dynamic-update-slice_fusion.2
  164.5 0.6 fusion.33
  165.0 1.4 bitcast_dynamic-update-slice_fusion.2
  166.5 19.7 %custom-call.19 = f32[2,128,128]{1,2,0:T(8,128)S(1)} custom-call(f32[2,128,128]{2,1,0:T(8,128)S(1)} %get-tuple-element.10), custom_call_target="InvertDiagBlocksLowerTriangular" | custom-call | tf_op jit(solution)/shard_map/jit(_solve_triangular)/triangular_solve | solution.py:22
  186.1 0.0 copy-done.3
  186.2 0.4 fusion.5
  186.6 0.4 convolution_subtract_fusion.2
  187.0 0.4 fusion.14
  187.4 0.0 copy-start.2
  187.4 1.1 fusion.3
  188.5 0.0 copy-start.1
  188.5 1.8 convolution_subtract_fusion.1
  190.4 1.1 fusion.13
  191.4 0.0 copy-done.2
  191.5 0.0 copy-done.1
  191.5 5.2 %convolution_subtract_fusion = f32[2048,512]{1,0:T(8,128)} fusion(f32[2048,512]{1,0:T(8,128)S(1)} %copy-done.1, f32[256,512]{1,0:T(8,128)S(1)} %pad_maximum_fusion, f32[128,2048]{1,0:T(8,128)S(1)} %fusion.13, f32[128,2048]{1,0:T(8,128)S(1)} %fusion.3), kind=kOutput, calls=%fused_computation.2 | convolution fusion | flops 3222798336 | bytes 11010048 | tf_op jit(solution)/shard_map/dot_general | solution.py:18
  (10 shorter events, 0.2 us)
Async XLA Ops:
  7.2 27.7 %all-gather.2.cloned.1.call-start = ((), (), s32[]{:S(2)}) async-start(), calls=%async_computation | async-start | bytes 2621440 | tf_op jit(solution)/shard_map/all_gather | solution.py:26
  7.9 115.5 %all-reduce.4.cloned.1.call-start = ((), (), s32[]{:S(2)}) async-start(), calls=%async_computation.1 | async-start | bytes 1572864 | tf_op jit(solution)/shard_map/psum | solution.py:27
  34.8 6.5 %copy-start = (f32[2048,256]{1,0:T(8,128)S(1)}, f32[2048,256]{1,0:T(8,128)}, u32[]{:S(2)}) copy-start(f32[2048,256]{1,0:T(8,128)} %all-gather.2.cloned.1.call-done) | copy-start | bytes 6291460
  124.5 61.6 %copy-start.3 = (f32[256,512]{1,0:T(8,128)S(1)}, f32[256,512]{1,0:T(8,128)}, u32[]{:S(2)}) copy-start(f32[256,512]{1,0:T(8,128)} %get-tuple-element.23) | copy-start | bytes 1572868
  187.4 4.0 %copy-start.2 = (f32[256,512]{1,0:T(8,128)}, f32[256,512]{1,0:T(8,128)S(1)}, u32[]{:S(2)}) copy-start(f32[256,512]{1,0:T(8,128)S(1)} %pad_maximum_fusion) | copy-start | bytes 1572868
  188.5 2.9 %copy-start.1 = (f32[2048,512]{1,0:T(8,128)S(1)}, f32[2048,512]{1,0:T(8,128)}, u32[]{:S(2)}) copy-start(f32[2048,512]{1,0:T(8,128)} %param.3) | copy-start | bytes 12582916
Sparse Core Ops, SparseCore 0:
  9.5 25.2 all-gather.1
  48.2 75.2 all-reduce.3
where the time goes:
time: 204 us
  waiting for transfers between devices  103 us (50%)
  other arithmetic  54.9 us (27%)
  matrix products  24 us (12%)
  between operations  15.5 us (8%)
  local copies, waits for them, and re-layouts  6.04 us (3%)
    psum x1, waiting for transfers between devices, shards(): lax.psum((inner(block, block), inner(block, trailing)), 'rows')  75.3 us
    another operation x6, other arithmetic, shards(): rfactor = jnp.linalg.cholesky(gram).T  34.1 us
    all_gather x1, waiting for transfers between devices, shards(): block = lax.all_gather(panel, 'cols', axis=0, tiled=True)  26.9 us
    another operation x4, other arithmetic, lower_solve(): return jax.scipy.linalg.solve_triangular(rfactor.T, right, lower=True)  19.8 us
    dot_general x2, matrix products, inner(): lax.dot_general(left, right, (((0,), (0,)), ((), ())), precision=lax.Prec...  13.2 us
    dot_general x1, matrix products, times(): jnp.dot(left, right, precision=lax.Precision.HIGHEST, preferred_element_t...  5.22 us
    another operation x6, matrix products, lower_solve(): return jax.scipy.linalg.solve_triangular(rfactor.T, right, lower=True)  5.17 us
  transfers between devices with their start and end apart: 2, of which 2 were waited for; matrix products, arithmetic and copies ran while one was open for 0% of the time, Pallas kernels for 0%

commit v1 on v0

v1 whole, which is shorter than its diff:
```python
import functools

import jax
import jax.numpy as jnp
from jax import lax
from jax.experimental import pallas as pl
from jax.experimental.pallas import tpu as pltpu
from jax.sharding import PartitionSpec as P

MESH = pl.DeviceIdType.MESH
F32 = jnp.float32
LANES = 128
SUBLANES = 8
STRIP = 32


def contract(left, right, dims):
    return lax.dot_general(
        left, right, (dims, ((), ())), precision=lax.Precision.HIGHEST, preferred_element_type=F32
    )


def halves(x):
    high = x.astype(jnp.bfloat16)
    return high, (x - high.astype(F32)).astype(jnp.bfloat16)


def contract3(left, right, dims):
    dot = functools.partial(
        lax.dot_general, dimension_numbers=(dims, ((), ())), preferred_element_type=F32
    )
    (lh, ll), (rh, rl) = left, right
    return dot(lh, rh) + (dot(lh, rl) + dot(ll, rh))


def factor_strip(start, g_ref, r_ref, y_ref):
    n = g_ref.shape[0]
    row = lax.broadcasted_iota(jnp.int32, (STRIP, LANES), 0)
    col = lax.broadcasted_iota(jnp.int32, (STRIP, LANES), 1)
    rows = pl.ds(start, STRIP)
    parts = []
    first = start // LANES * LANES
    for at in range(first, n, LANES):
        parts.append((r_ref, at, g_ref[rows, at : at + LANES]))
    for at in range(0, start + STRIP, LANES):
        parts.append((y_ref, at, jnp.where(col + at == row + start, 1.0, 0.0).astype(F32)))
    if start:
        left = r_ref[0:start, first : first + LANES][:, start - first : start - first + STRIP]
        right = jnp.concatenate([ref[0:start, at : at + LANES] for ref, at, _ in parts], axis=1)
        done = contract(left, right, ((0,), (0,)))
        parts = [
            (ref, at, x - done[:, LANES * i : LANES * (i + 1)]) for i, (ref, at, x) in enumerate(parts)
        ]
    values = [x for _, _, x in parts]
    shift = start - first
    columns = [
        jnp.broadcast_to(values[0][:, shift + i : shift + i + 1], (STRIP, LANES)) for i in range(STRIP)
    ]
    for i in range(STRIP):
        inverse = lax.rsqrt(columns[i][i : i + 1, :])
        scaled = columns[i] * inverse
        for k in range(i + 1, STRIP):
            base = k // SUBLANES * SUBLANES
            low = columns[k][base:] - scaled[base:] * scaled[k : k + 1, :]
            columns[k] = low if base == 0 else jnp.concatenate([columns[k][:base], low], axis=0)
        factor = jnp.where(row > i, scaled, 0.0)
        for v, x in enumerate(values):
            pivot = x[i : i + 1, :] * inverse
            values[v] = jnp.where(row == i, pivot, x - factor * pivot)
    for (ref, at, _), x in zip(parts, values):
        if ref is r_ref:
            x = jnp.where(col + at >= row + start, x, 0.0)
        else:
            x = jnp.where(col + at <= row + start, x, 0.0)
        ref[rows, at : at + LANES] = x


def gather_and_factor(
    nrows, ncols, panel_ref, trailing_ref, r_ref, y_ref, cross_ref, block_ref,
    held, pieces, gram, gram_in, gram_sum, share, share_in, total,
    load_sem, piece_send, piece_recv, gram_sem, share_sem,
):
    r, c = lax.axis_index("rows"), lax.axis_index("cols")
    count = nrows * ncols
    me = r * ncols + c
    depth, n = panel_ref.shape
    width = trailing_ref.shape[1]
    owners = min(count, n // SUBLANES)
    piece = n // owners
    row_owners = min(nrows, n // SUBLANES)
    row_piece = n // row_owners

    load = pltpu.make_async_copy(trailing_ref, held, load_sem)
    load.start()
    pieces[c] = panel_ref[...]

    bits = [1 << b for b in reversed(range(ncols.bit_length() - 1))]
    known = [0]
    index = 0
    sent = []

    def pass_on(offsets, bit):
        nonlocal index
        out = []
        for offset in offsets:
            slot = jnp.bitwise_xor(c, offset) if offset else c
            source = pieces.at[slot] if offset else panel_ref
            copy = pltpu.make_async_remote_copy(
                src_ref=source, dst_ref=pieces.at[slot],
                send_sem=piece_send.at[index], recv_sem=piece_recv.at[index],
                device_id=(r, jnp.bitwise_xor(c, bit)), device_id_type=MESH,
            )
            copy.start()
            sent.append(copy)
            out.append((offset ^ bit, copy))
            index += 1
        return out

    arrivals = {bit: pass_on([0], bit) for bit in bits}

    gram[...] = contract(panel_ref[...], panel_ref[...], ((0,), (0,)))

    def spread(k, action):
        target = lax.rem(me + k, count)
        copy = pltpu.make_async_remote_copy(
            src_ref=gram.at[pl.ds(pl.multiple_of(target * piece, SUBLANES), piece)],
            dst_ref=gram_in.at[me],
            send_sem=gram_sem.at[0], recv_sem=gram_sem.at[1],
            device_id=(lax.div(target, ncols), lax.rem(target, ncols)), device_id_type=MESH,
        )
        if owners == count:
            action(copy)
        else:
            pl.when(target < owners)(lambda: action(copy))

    def each(n_steps, f):
        def step(k, carry):
            f(k)
            return carry
        lax.fori_loop(1, n_steps, step, 0)

    each(count, lambda k: spread(k, lambda copy: copy.start()))

    for at, bit in enumerate(bits):
        for offset, copy in arrivals[bit]:
            copy.wait_recv()
        for later in bits[at + 1 :]:
            arrivals[later] += pass_on([offset for offset, _ in arrivals[bit]], later)

    def own(body):
        if owners == count:
            body()
        else:
            pl.when(me < owners)(body)

    mine = pl.ds(pl.multiple_of(lax.rem(me, owners) * piece, SUBLANES), piece)

    @own
    def _():
        gram_in[me] = gram[mine, :]
        others = gram_in.at[pl.ds(0, count - 1)]
        pltpu.make_async_copy(others, others, gram_sem.at[1]).wait()
        gram_sum[mine, :] = jnp.sum(gram_in[...], axis=0)

        def give(k):
            target = lax.rem(me + k, count)
            pltpu.make_async_remote_copy(
                src_ref=gram_sum.at[mine], dst_ref=gram_sum.at[mine],
                send_sem=gram_sem.at[2], recv_sem=gram_sem.at[3],
                device_id=(lax.div(target, ncols), lax.rem(target, ncols)), device_id_type=MESH,
            ).start()

        each(count, give)

    load.wait()
    tile = 256
    share[...] = jnp.zeros_like(share)

    def multiply(i, carry):
        at = pl.ds(pl.multiple_of(i * tile, tile), tile)
        flat = pieces.reshape(ncols * depth, n)
        share[...] += contract3(halves(flat[at, :]), halves(held[at, :]), ((0,), (0,)))
        return carry

    lax.fori_loop(0, ncols * depth // tile, multiply, 0)

    def row_target(k):
        return lax.rem(r + k, nrows)

    def deal(k):
        target = row_target(k)

        def go():
            pltpu.make_async_remote_copy(
                src_ref=share.at[pl.ds(pl.multiple_of(target * row_piece, SUBLANES), row_piece)],
                dst_ref=share_in.at[r],
                send_sem=share_sem.at[0], recv_sem=share_sem.at[1],
                device_id=(target, c), device_id_type=MESH,
            ).start()

        if row_owners == nrows:
            go()
        else:
            pl.when(target < row_owners)(go)

    each(nrows, deal)
    block_out = pltpu.make_async_copy(pieces, block_ref, load_sem)
    block_out.start()

    def wait_pieces(ref, times, sem):
        if owners == count or times is None:
            pass

    def gram_arrived():
        if owners == count:
            rest = gram_sum.at[pl.ds(0, n - piece)]
            pltpu.make_async_copy(rest, rest, gram_sem.at[3]).wait()
        else:
            @pl.when(me < owners)
            def _():
                rest = gram_sum.at[pl.ds(0, n - piece)]
                pltpu.make_async_copy(rest, rest, gram_sem.at[3]).wait()

            @pl.when(me >= owners)
            def _():
                pltpu.make_async_copy(gram_sum, gram_sum, gram_sem.at[3]).wait()

    gram_arrived()
    strips = list(range(0, n, STRIP))
    half = len(strips) // 2
    for start in strips[:half]:
        factor_strip(start, gram_sum, r_ref, y_ref)

    def row_own(body):
        if row_owners == nrows:
            body()
        else:
            pl.when(r < row_owners)(body)

    my_rows = pl.ds(pl.multiple_of(lax.rem(r, row_owners) * row_piece, SUBLANES), row_piece)

    @row_own
    def _():
        share_in[r] = share[my_rows, :]
        others = share_in.at[pl.ds(0, nrows - 1)]
        pltpu.make_async_copy(others, others, share_sem.at[1]).wait()
        total[my_rows, :] = jnp.sum(share_in[...], axis=0)

        def give(k):
            pltpu.make_async_remote_copy(
                src_ref=total.at[my_rows], dst_ref=total.at[my_rows],
                send_sem=share_sem.at[2], recv_sem=share_sem.at[3],
                device_id=(row_target(k), c), device_id_type=MESH,
            ).start()

        each(nrows, give)

    for start in strips[half:]:
        if start >= LANES:
            r_ref[start : start + STRIP, 0 : start // LANES * LANES] = jnp.zeros(
                (STRIP, start // LANES * LANES), F32
            )
        factor_strip(start, gram_sum, r_ref, y_ref)
    for start in strips:
        edge = -(-(start + STRIP) // LANES) * LANES
        if edge < n:
            y_ref[start : start + STRIP, edge:n] = jnp.zeros((STRIP, n - edge), F32)

    if row_owners == nrows:
        rest = total.at[pl.ds(0, n - row_piece)]
        pltpu.make_async_copy(rest, rest, share_sem.at[3]).wait()
    else:
        @pl.when(r < row_owners)
        def _():
            rest = total.at[pl.ds(0, n - row_piece)]
            pltpu.make_async_copy(rest, rest, share_sem.at[3]).wait()

        @pl.when(r >= row_owners)
        def _():
            pltpu.make_async_copy(total, total, share_sem.at[3]).wait()
    cross_ref[...] = total[...]

    for copy in sent:
        copy.wait_send()
    for bit in bits[1:]:
        pass

    def sent_all(ref, size, sem, index, limit, last):
        if limit == last:
            gone = ref.at[pl.ds(0, (limit - 1) * size)]
            pltpu.make_async_copy(gone, gone, sem).wait()
        else:
            @pl.when(index < limit)
            def _():
                gone = ref.at[pl.ds(0, (limit - 1) * size)]
                pltpu.make_async_copy(gone, gone, sem).wait()

            @pl.when(index >= limit)
            def _():
                gone = ref.at[pl.ds(0, limit * size)]
                pltpu.make_async_copy(gone, gone, sem).wait()

    sent_all(gram, piece, gram_sem.at[0], me, owners, count)
    sent_all(share, row_piece, share_sem.at[0], r, row_owners, nrows)

    def given_all(ref, sem, index, limit, last):
        def body():
            gone = ref.at[pl.ds(0, last - 1)]
            pltpu.make_async_copy(gone, gone, sem).wait()

        if limit == last:
            body()
        else:
            pl.when(index < limit)(body)

    given_all(gram_in, gram_sem.at[2], me, owners, count)
    given_all(share_in, share_sem.at[2], r, row_owners, nrows)
    block_out.wait()


def update(r_ref, y_ref, cross_ref, block_ref, trailing_ref, r_out, projected_ref, updated_ref, high, low):
    @pl.when(pl.program_id(0) == 0)
    def _():
        r_out[...] = r_ref[...]
        projected = contract(y_ref[...], cross_ref[...], ((1,), (0,)))
        projected_ref[...] = projected
        high[...], low[...] = halves(contract(y_ref[...], projected, ((0,), (0,))))

    product = contract3(halves(block_ref[...]), (high[...], low[...]), ((1,), (0,)))
    updated_ref[...] = trailing_ref[...] - product


def solution(mesh):
    nrows, ncols = mesh.shape["rows"], mesh.shape["cols"]

    def shards(panel, trailing):
        depth, n = panel.shape
        height, width = trailing.shape
        count = nrows * ncols
        owners = min(count, n // SUBLANES)
        row_owners = min(nrows, n // SUBLANES)
        vmem = pl.BlockSpec(memory_space=pltpu.VMEM)
        hbm = pl.BlockSpec(memory_space=pl.ANY)
        r, y, cross, block = pl.pallas_call(
            functools.partial(gather_and_factor, nrows, ncols),
            name="gather_and_factor",
            out_shape=(
                jax.ShapeDtypeStruct((n, n), F32),
                jax.ShapeDtypeStruct((n, n), F32),
                jax.ShapeDtypeStruct((n, width), F32),
                jax.ShapeDtypeStruct((ncols, depth, n), F32),
            ),
            in_specs=[vmem, hbm],
            out_specs=(vmem, vmem, vmem, hbm),
            scratch_shapes=[
                pltpu.VMEM((height, width), F32),
                pltpu.VMEM((ncols, depth, n), F32),
                pltpu.VMEM((n, n), F32),
                pltpu.VMEM((count, n // owners, n), F32),
                pltpu.VMEM((n, n), F32),
                pltpu.VMEM((n, width), F32),
                pltpu.VMEM((nrows, n // row_owners, width), F32),
                pltpu.VMEM((n, width), F32),
                pltpu.SemaphoreType.DMA,
                pltpu.SemaphoreType.DMA((ncols - 1,)),
                pltpu.SemaphoreType.DMA((ncols - 1,)),
                pltpu.SemaphoreType.DMA((4,)),
                pltpu.SemaphoreType.DMA((4,)),
            ],
            compiler_params=pltpu.CompilerParams(has_side_effects=True, vmem_limit_bytes=40 << 20),
        )(panel, trailing)
        block = block.reshape(height, n)
        tile = min(height, 512)
        whole = lambda *shape: pl.BlockSpec(shape, lambda i: (0, 0))
        tall = lambda wide: pl.BlockSpec((tile, wide), lambda i: (i, 0))
        return pl.pallas_call(
            update,
            name="update",
            grid=(height // tile,),
            out_shape=(
                jax.ShapeDtypeStruct((n, n), F32),
                jax.ShapeDtypeStruct((n, width), F32),
                jax.ShapeDtypeStruct((height, width), F32),
            ),
            in_specs=[whole(n, n), whole(n, n), whole(n, width), tall(n), tall(width)],
            out_specs=(whole(n, n), whole(n, width), tall(width)),
            scratch_shapes=[pltpu.VMEM((n, width), jnp.bfloat16)] * 2,
            compiler_params=pltpu.CompilerParams(vmem_limit_bytes=32 << 20),
        )(r, y, cross, block, trailing)

    placed = (P(("rows", "cols"), None), P("rows", "cols"))
    return jax.shard_map(
        shards,
        mesh=mesh,
        in_specs=placed,
        out_specs=(P(), P(None, "cols"), P("rows", "cols")),
        check_vma=False,
    )
```

time: 204 us -> 65.5 us (0.32)
  the two profiles are of different devices: /device:TPU:0 before, /device:TPU:29 now
where the time goes in v1:
time: 65.5 us; the launch traced here: 65.3 us
  Pallas kernels  61.4 us (94%)
  local copies, waits for them, and re-layouts  3.22 us (5%)
    pallas_call x1, Pallas kernels, shards(): pl.pallas_call(functools.partial(gather_and_factor, nrows, ncols), name='...  56.4 us
    pallas_call x1, Pallas kernels, shards(): pl.pallas_call(update, name='update', grid=(height // tile,), out_shape=(...  5 us
    unnamed x4, local copies, waits for them, and re-layouts  3.22 us

profile of v1, /device:TPU:29, one launch (start us, length us, event | category | flops | bytes accessed | tf_op | source)
XLA Modules:
  0.0 65.3 jit_solution(4504793298641562932)
XLA Ops:
  0.6 0.0 copy-start
  0.6 2.2 %copy-done = f32[2048,512]{1,0:T(8,128)S(1)} copy-done((f32[2048,512]{1,0:T(8,128)S(1)}, f32[2048,512]{1,0:T(8,128)}, u32[]{:S(2)}) %copy-start) | copy-done | bytes 4194328
  2.8 0.0 copy-start.1
  2.8 1.0 %copy-done.1 = f32[512,256]{1,0:T(8,128)S(1)} copy-done((f32[512,256]{1,0:T(8,128)S(1)}, f32[512,256]{1,0:T(8,128)}, u32[]{:S(2)}) %copy-start.1) | copy-done | bytes 524312
  3.9 56.4 %gather_and_factor.1 = (f32[256,256]{1,0:T(8,128)S(1)}, f32[256,256]{1,0:T(8,128)S(1)}, f32[256,512]{1,0:T(8,128)S(1)}, f32[4,512,256]{2,1,0:T(8,128)S(1)}) custom-call(f32[512,256]{1,0:T(8,128)S(1)} %copy-done.1, f32[2048,512]{1,0:T(8,128)S(1)} %copy-done), custom_call_target="tpu_custom_call" | custom-call | tf_op jit(solution)/shard_map/gather_and_factor/pallas_call | solution.py:344
  60.3 5.0 %update.1 = (f32[256,256]{1,0:T(8,128)}, f32[256,512]{1,0:T(8,128)}, f32[2048,512]{1,0:T(8,128)}) custom-call(f32[256,256]{1,0:T(8,128)S(1)} %get-tuple-element.7.r_ref, f32[256,256]{1,0:T(8,128)S(1)} %get-tuple-element.8.y_ref, f32[256,512]{1,0:T(8,128)S(1)} %get-tuple-element.9.cross_ref, f32[2048,256]{1,0:T(8,128)S(1)} %bitcast.1, f32[2048,512]{1,0:T(8,128)S(1)} %copy-done), custom_call_target="tpu_custom_call" | custom-call | tf_op jit(solution)/shard_map/update/pallas_call | solution.py:376
Async XLA Ops:
  0.6 2.2 %copy-start = (f32[2048,512]{1,0:T(8,128)S(1)}, f32[2048,512]{1,0:T(8,128)}, u32[]{:S(2)}) copy-start(f32[2048,512]{1,0:T(8,128)} %trailing_ref.3) | copy-start | bytes 12582916
  2.8 1.0 %copy-start.1 = (f32[512,256]{1,0:T(8,128)S(1)}, f32[512,256]{1,0:T(8,128)}, u32[]{:S(2)}) copy-start(f32[512,256]{1,0:T(8,128)} %panel_ref.1) | copy-start | bytes 1572868

commit v2 on v0

v2 whole, which is shorter than its diff:
```python
import functools

import jax
import jax.numpy as jnp
from jax import lax
from jax.experimental import pallas as pl
from jax.experimental.pallas import tpu as pltpu
from jax.sharding import PartitionSpec as P

MESH = pl.DeviceIdType.MESH
F32 = jnp.float32
LANES = 128
SUBLANES = 8
STRIP = 32
CHUNK = 128


def contract(left, right, dims):
    return lax.dot_general(
        left, right, (dims, ((), ())), precision=lax.Precision.HIGHEST, preferred_element_type=F32
    )


def halves(x):
    high = x.astype(jnp.bfloat16)
    return high, (x - high.astype(F32)).astype(jnp.bfloat16)


def contract3(left, right, dims):
    dot = functools.partial(
        lax.dot_general, dimension_numbers=(dims, ((), ())), preferred_element_type=F32
    )
    (lh, ll), (rh, rl) = left, right
    return dot(lh, rh) + (dot(lh, rl) + dot(ll, rh))


def factor_strip(start, g_ref, r_ref, y_ref):
    n = g_ref.shape[0]
    row = lax.broadcasted_iota(jnp.int32, (STRIP, LANES), 0)
    col = lax.broadcasted_iota(jnp.int32, (STRIP, LANES), 1)
    rows = pl.ds(start, STRIP)
    parts = []
    first = start // LANES * LANES
    for at in range(first, n, LANES):
        parts.append((r_ref, at, g_ref[rows, at : at + LANES]))
    for at in range(0, start + STRIP, LANES):
        parts.append((y_ref, at, jnp.where(col + at == row + start, 1.0, 0.0).astype(F32)))
    if start:
        left = r_ref[0:start, first : first + LANES][:, start - first : start - first + STRIP]
        right = jnp.concatenate([ref[0:start, at : at + LANES] for ref, at, _ in parts], axis=1)
        done = contract(left, right, ((0,), (0,)))
        parts = [
            (ref, at, x - done[:, LANES * i : LANES * (i + 1)]) for i, (ref, at, x) in enumerate(parts)
        ]
    values = [x for _, _, x in parts]
    shift = start - first
    columns = [
        jnp.broadcast_to(values[0][:, shift + i : shift + i + 1], (STRIP, LANES)) for i in range(STRIP)
    ]
    for i in range(STRIP):
        inverse = lax.rsqrt(columns[i][i : i + 1, :])
        scaled = columns[i] * inverse
        for k in range(i + 1, STRIP):
            base = k // SUBLANES * SUBLANES
            low = columns[k][base:] - scaled[base:] * scaled[k : k + 1, :]
            columns[k] = low if base == 0 else jnp.concatenate([columns[k][:base], low], axis=0)
        factor = jnp.where(row > i, scaled, 0.0)
        for v, x in enumerate(values):
            pivot = x[i : i + 1, :] * inverse
            values[v] = jnp.where(row == i, pivot, x - factor * pivot)
    for (ref, at, _), x in zip(parts, values):
        if ref is r_ref:
            x = jnp.where(col + at >= row + start, x, 0.0)
        else:
            x = jnp.where(col + at <= row + start, x, 0.0)
        ref[rows, at : at + LANES] = x


class Direct:
    def __init__(self, members, member, device, size, source, landing, result, base, sems):
        self.members, self.member, self.device = members, member, device
        self.source, self.landing, self.result, self.base, self.sems = source, landing, result, base, sems
        self.owners = min(members, size // SUBLANES)
        self.piece = size // self.owners

    def rows(self, index, base=0):
        return pl.ds(pl.multiple_of(base + index * self.piece, SUBLANES), self.piece)

    def if_owner(self, index, body):
        if self.owners == self.members:
            body()
        else:
            pl.when(index < self.owners)(body)

    def each(self, body):
        def step(k, carry):
            body(lax.rem(self.member + k, self.members))
            return carry

        lax.fori_loop(1, self.members, step, 0, unroll=self.members <= 4)

    def wait(self, ref, sem):
        pltpu.make_async_copy(ref, ref, sem).wait()

    def wait_parts(self, sem):
        def whole(parts):
            self.wait(self.result.at[pl.ds(0, parts * self.piece)], sem)

        if self.owners == self.members:
            whole(self.owners - 1)
        else:
            pl.when(self.member < self.owners)(lambda: whole(self.owners - 1))
            pl.when(self.member >= self.owners)(lambda: whole(self.owners))

    def scatter(self):
        def send(target):
            self.if_owner(target, lambda: pltpu.make_async_remote_copy(
                src_ref=self.source.at[self.rows(target)], dst_ref=self.landing.at[self.member],
                send_sem=self.sems.at[0], recv_sem=self.sems.at[1],
                device_id=self.device(target), device_id_type=MESH,
            ).start())

        self.each(send)

    def reduce(self):
        @functools.partial(self.if_owner, self.member)
        def _():
            index = lax.rem(self.member, self.owners)
            mine = self.rows(index, self.base)
            self.landing[self.member] = self.source[self.rows(index), :]
            self.wait(self.landing.at[pl.ds(0, self.members - 1)], self.sems.at[1])
            self.result[mine, :] = jnp.sum(self.landing[...], axis=0)
            self.each(lambda target: pltpu.make_async_remote_copy(
                src_ref=self.result.at[mine], dst_ref=self.result.at[mine],
                send_sem=self.sems.at[2], recv_sem=self.sems.at[3],
                device_id=self.device(target), device_id_type=MESH,
            ).start())

    def arrived(self):
        self.wait_parts(self.sems.at[3])

    def finish(self):
        self.wait_parts(self.sems.at[0])
        self.if_owner(self.member, lambda: self.wait(
            self.landing.at[pl.ds(0, self.members - 1)], self.sems.at[2]))


class Pair:
    def __init__(self, side, device, half, source, base, landing, kept, sems):
        self.device, self.source, self.landing, self.kept, self.sems = device, source, landing, kept, sems
        self.mine = pl.ds(pl.multiple_of(base + side * half, SUBLANES), half)
        self.other = pl.ds(pl.multiple_of(base + (1 - side) * half, SUBLANES), half)

    def scatter(self):
        self.out = pltpu.make_async_remote_copy(
            src_ref=self.source.at[self.other], dst_ref=self.landing,
            send_sem=self.sems.at[0], recv_sem=self.sems.at[1],
            device_id=self.device, device_id_type=MESH,
        )
        self.out.start()

    def reduce(self):
        self.out.wait_recv()
        self.kept[...] = self.source[self.mine, :] + self.landing[...]

    def gather(self, result):
        self.back = pltpu.make_async_remote_copy(
            src_ref=result.at[self.mine], dst_ref=result.at[self.mine],
            send_sem=self.sems.at[2], recv_sem=self.sems.at[3],
            device_id=self.device, device_id_type=MESH,
        )
        self.back.start()

    def arrived(self):
        self.back.wait_recv()

    def finish(self):
        self.out.wait_send()
        self.back.wait_send()


def gather_and_factor(
    nrows, ncols, panel_ref, trailing_ref, r_ref, y_ref, cross_ref, block_ref,
    held, high, low, pieces, gram, gram_near, gram_pair, gram_in, gram_sum,
    share, share_near, share_pair, share_in, total,
    load_sem, piece_send, piece_recv, gram_pair_sem, gram_sem, share_pair_sem, share_sem,
):
    r, c = lax.axis_index("rows"), lax.axis_index("cols")
    depth, n = panel_ref.shape
    chunks = n // CHUNK

    own_load = pltpu.make_async_copy(panel_ref, pieces.at[c], load_sem.at[0])
    own_load.start()
    load = pltpu.make_async_copy(trailing_ref, held, load_sem.at[1])
    load.start()
    own_load.wait()

    bits = [1 << b for b in reversed(range(ncols.bit_length() - 1))]
    sent = []

    def pass_on(offset, bit, chunk):
        slot = jnp.bitwise_xor(c, offset)
        view = pieces.at[slot, :, pl.ds(chunk * CHUNK, CHUNK)]
        copy = pltpu.make_async_remote_copy(
            src_ref=view, dst_ref=view,
            send_sem=piece_send.at[len(sent)], recv_sem=piece_recv.at[len(sent)],
            device_id=(r, jnp.bitwise_xor(c, bit)), device_id_type=MESH,
        )
        copy.start()
        sent.append(copy)
        return offset ^ bit, copy

    coming = {(bit, chunk): [pass_on(0, bit, chunk)] for chunk in range(chunks) for bit in bits}

    gram[...] = contract(pieces[c], pieces[c], ((0,), (0,)))
    side, wide = lax.rem(c, 2), ncols // 2
    gram_halves = Pair(side, (r, jnp.bitwise_xor(c, 1)), n // 2, gram, 0, gram_near, gram_pair, gram_pair_sem)
    gram_halves.scatter()
    gram_all = Direct(
        nrows * wide, r * wide + lax.div(c, 2),
        lambda t: (lax.div(t, wide), lax.rem(t, wide) * 2 + side),
        n // 2, gram_pair, gram_in, gram_sum, side * (n // 2), gram_sem,
    )
    upper = lax.rem(r, 2)
    pairs, groups = [], []
    for h in range(chunks):
        half = CHUNK // 2
        pairs.append(Pair(
            upper, (jnp.bitwise_xor(r, 1), c), half, share, h * CHUNK,
            share_near.at[h], share_pair.at[h], share_pair_sem.at[h],
        ))
        groups.append(Direct(
            nrows // 2, lax.div(r, 2), lambda t: (t * 2 + upper, c),
            half, share_pair.at[h], share_in.at[h], total, h * CHUNK + upper * half, share_sem.at[h],
        ))

    load.wait()

    def split(i, carry):
        at = pl.ds(pl.multiple_of(i * LANES, LANES), LANES)
        high[at, :], low[at, :] = halves(held[at, :])
        return carry

    lax.fori_loop(0, held.shape[0] // LANES, split, 0)
    gram_halves.reduce()
    gram_all.scatter()

    def multiply(offset, h, first=False):
        slot = jnp.bitwise_xor(c, offset)
        at = pl.ds(pl.multiple_of(slot * depth, LANES), depth)
        mine = slice(h * CHUNK, (h + 1) * CHUNK)
        product = contract3(halves(pieces[slot, :, mine]), (high[at, :], low[at, :]), ((0,), (0,)))
        share[mine, :] = product if first else share[mine, :] + product

    for h in range(chunks):
        multiply(0, h, True)
    for h in range(chunks):
        offset, copy = coming[bits[-1], h].pop(0)
        copy.wait_recv()
        multiply(offset, h)

    def take(h):
        for at, bit in enumerate(bits):
            for offset, copy in coming[bit, h]:
                copy.wait_recv()
                for later in bits[at + 1 :]:
                    coming[later, h].append(pass_on(offset, later, h))
                multiply(offset, h)
        pairs[h].scatter()

    strips = list(range(0, n, STRIP))

    def factor(some):
        for start in some:
            if start >= LANES:
                r_ref[start : start + STRIP, 0 : start // LANES * LANES] = jnp.zeros(
                    (STRIP, start // LANES * LANES), F32
                )
            edge = -(-(start + STRIP) // LANES) * LANES
            if edge < n:
                y_ref[start : start + STRIP, edge:n] = jnp.zeros((STRIP, n - edge), F32)
            factor_strip(start, gram_sum, r_ref, y_ref)

    take(0)
    gram_all.reduce()
    for h in range(1, chunks):
        pairs[h - 1].reduce()
        groups[h - 1].scatter()
        take(h)
        groups[h - 1].reduce()
    block_out = pltpu.make_async_copy(pieces, block_ref, load_sem.at[1])
    block_out.start()
    gram_all.arrived()
    gram_halves.gather(gram_sum)
    pairs[-1].reduce()
    groups[-1].scatter()
    gram_halves.arrived()
    half = len(strips) // 2
    factor(strips[:half])
    groups[-1].reduce()
    for h in range(chunks - 1):
        groups[h].arrived()
        pairs[h].gather(total)
    factor(strips[half:])
    groups[-1].arrived()
    pairs[-1].gather(total)
    for pair in pairs:
        pair.arrived()
    cross_ref[...] = total[...]
    for copy in sent:
        copy.wait_send()
    for exchange in [gram_halves, gram_all] + pairs + groups:
        exchange.finish()
    block_out.wait()


def update(r_ref, y_ref, cross_ref, block_ref, trailing_ref, r_out, projected_ref, updated_ref, high, low):
    @pl.when(pl.program_id(0) == 0)
    def _():
        r_out[...] = r_ref[...]
        projected = contract(y_ref[...], cross_ref[...], ((1,), (0,)))
        projected_ref[...] = projected
        high[...], low[...] = halves(contract(y_ref[...], projected, ((0,), (0,))))

    product = contract3(halves(block_ref[...]), (high[...], low[...]), ((1,), (0,)))
    updated_ref[...] = trailing_ref[...] - product


def solution(mesh):
    nrows, ncols = mesh.shape["rows"], mesh.shape["cols"]

    def shards(panel, trailing):
        depth, n = panel.shape
        height, width = trailing.shape
        chunks = n // CHUNK
        half = CHUNK // 2
        group = nrows * ncols // 2
        vmem = pl.BlockSpec(memory_space=pltpu.VMEM)
        hbm = pl.BlockSpec(memory_space=pl.ANY)
        r, y, cross, block = pl.pallas_call(
            functools.partial(gather_and_factor, nrows, ncols),
            name="gather_and_factor",
            out_shape=(
                jax.ShapeDtypeStruct((n, n), F32),
                jax.ShapeDtypeStruct((n, n), F32),
                jax.ShapeDtypeStruct((n, width), F32),
                jax.ShapeDtypeStruct((ncols, depth, n), F32),
            ),
            in_specs=[hbm, hbm],
            out_specs=(vmem, vmem, vmem, hbm),
            scratch_shapes=[
                pltpu.VMEM((height, width), F32),
                pltpu.VMEM((height, width), jnp.bfloat16),
                pltpu.VMEM((height, width), jnp.bfloat16),
                pltpu.VMEM((ncols, depth, n), F32),
                pltpu.VMEM((n, n), F32),
                pltpu.VMEM((n // 2, n), F32),
                pltpu.VMEM((n // 2, n), F32),
                pltpu.VMEM((group, n // 2 // min(group, n // 2 // SUBLANES), n), F32),
                pltpu.VMEM((n, n), F32),
                pltpu.VMEM((n, width), F32),
                pltpu.VMEM((chunks, half, width), F32),
                pltpu.VMEM((chunks, half, width), F32),
                pltpu.VMEM((chunks, nrows // 2, half // min(nrows // 2, half // SUBLANES), width), F32),
                pltpu.VMEM((n, width), F32),
                pltpu.SemaphoreType.DMA((2,)),
                pltpu.SemaphoreType.DMA(((ncols - 1) * chunks,)),
                pltpu.SemaphoreType.DMA(((ncols - 1) * chunks,)),
                pltpu.SemaphoreType.DMA((4,)),
                pltpu.SemaphoreType.DMA((4,)),
                pltpu.SemaphoreType.DMA((chunks, 4)),
                pltpu.SemaphoreType.DMA((chunks, 4)),
            ],
            compiler_params=pltpu.CompilerParams(has_side_effects=True, vmem_limit_bytes=67043328),
        )(panel, trailing)
        block = block.reshape(height, n)
        tile = min(height, 512)
        whole = lambda *shape: pl.BlockSpec(shape, lambda i: (0, 0))
        tall = lambda wide: pl.BlockSpec((tile, wide), lambda i: (i, 0))
        return pl.pallas_call(
            update,
            name="update",
            grid=(height // tile,),
            out_shape=(
                jax.ShapeDtypeStruct((n, n), F32),
                jax.ShapeDtypeStruct((n, width), F32),
                jax.ShapeDtypeStruct((height, width), F32),
            ),
            in_specs=[whole(n, n), whole(n, n), whole(n, width), tall(n), tall(width)],
            out_specs=(whole(n, n), whole(n, width), tall(width)),
            scratch_shapes=[pltpu.VMEM((n, width), jnp.bfloat16)] * 2,
            compiler_params=pltpu.CompilerParams(vmem_limit_bytes=32 << 20),
        )(r, y, cross, block, trailing)

    placed = (P(("rows", "cols"), None), P("rows", "cols"))
    return jax.shard_map(
        shards,
        mesh=mesh,
        in_specs=placed,
        out_specs=(P(), P(None, "cols"), P("rows", "cols")),
        check_vma=False,
    )
```

time: 204 us -> 61.3 us (0.30)
  waiting for transfers between devices: 103 us -> 0 us
  other arithmetic: 54.9 us -> 0 us
  Pallas kernels: 0 us -> 53.6 us
  matrix products: 24 us -> 0 us
  between operations: 15.5 us -> 0.65 us
    psum x1 -> x0, waiting for transfers between devices: 75.3 us -> none  [shards(): lax.psum((inner(block, block), inner(block, trailing)), 'rows')]
    another operation x10 -> x0, other arithmetic: 53.8 us -> none  [the longest x6 34.1 us: shards(): rfactor = jnp.linalg.cholesky(gram).T]
    pallas_call x0 -> x2, Pallas kernels: none -> 53.6 us  [the longest x1 48.7 us: shards(): pl.pallas_call(functools.partial(gather_and_factor, nrows, ncols), name='...]
    all_gather x1 -> x0, waiting for transfers between devices: 26.9 us -> none  [shards(): block = lax.all_gather(panel, 'cols', axis=0, tiled=True)]
    dot_general x3 -> x0, matrix products: 18.4 us -> none  [the longest x2 13.2 us: inner(): lax.dot_general(left, right, (((0,), (0,)), ((), ())), precision=lax.Prec...]
    unnamed x9 -> x10, local copies, waits for them, and re-layouts: 0.86 us -> 6.71 us
    another operation x8 -> x0, matrix products: 5.64 us -> none  [the longest x6 5.17 us: lower_solve(): return jax.scipy.linalg.solve_triangular(rfactor.T, right, lower=True)]
    another operation x9 -> x0, local copies, waits for them, and re-layouts: 4.1 us -> none
  transfers between devices with their start and end apart: 2 -> 0, of which waited for: 2 -> 0; matrix products, arithmetic and copies ran while one was open for 0% -> 0% of each run, Pallas kernels for 0% -> 0%
where the time goes in v2:
time: 61.3 us; the launch traced here: 61 us
  Pallas kernels  53.6 us (87%)
  local copies, waits for them, and re-layouts  6.71 us (11%)
  between operations  0.65 us (1%)
    pallas_call x1, Pallas kernels, shards(): pl.pallas_call(functools.partial(gather_and_factor, nrows, ncols), name='...  48.7 us
    unnamed x10, local copies, waits for them, and re-layouts  6.71 us
    pallas_call x1, Pallas kernels, shards(): pl.pallas_call(update, name='update', grid=(height // tile,), out_shape=(...  4.97 us

profile of v2, /device:TPU:0, one launch (start us, length us, event | category | flops | bytes accessed | tf_op | source)
XLA Modules:
  0.0 61.0 jit_solution(8590986204265310696)
XLA Ops:
  0.6 48.7 %gather_and_factor.1 = (f32[256,256]{1,0:T(8,128)}, f32[256,256]{1,0:T(8,128)}, f32[256,512]{1,0:T(8,128)}, f32[4,512,256]{2,1,0:T(8,128)}) custom-call(f32[512,256]{1,0:T(8,128)} %panel_ref.1, f32[2048,512]{1,0:T(8,128)} %trailing_ref.3), custom_call_target="tpu_custom_call" | custom-call | tf_op jit(solution)/shard_map/gather_and_factor/pallas_call | solution.py:340
  49.3 0.0 copy-start
  49.3 2.2 %copy-done = f32[2048,512]{1,0:T(8,128)S(1)} copy-done((f32[2048,512]{1,0:T(8,128)S(1)}, f32[2048,512]{1,0:T(8,128)}, u32[]{:S(2)}) %copy-start) | copy-done | bytes 4194328
  51.5 0.0 copy-start.1
  51.5 1.6 %copy-done.1 = f32[4,512,256]{2,1,0:T(8,128)S(1)} copy-done((f32[4,512,256]{2,1,0:T(8,128)S(1)}, f32[4,512,256]{2,1,0:T(8,128)}, u32[]{:S(2)}) %copy-start.1) | copy-done | bytes 2097176
  53.1 0.0 copy-start.2
  53.1 1.0 %copy-done.2 = f32[256,512]{1,0:T(8,128)S(1)} copy-done((f32[256,512]{1,0:T(8,128)S(1)}, f32[256,512]{1,0:T(8,128)}, u32[]{:S(2)}) %copy-start.2) | copy-done | bytes 524312
  54.1 0.0 copy-start.3
  54.1 0.9 %copy-done.3 = f32[256,256]{1,0:T(8,128)S(1)} copy-done((f32[256,256]{1,0:T(8,128)S(1)}, f32[256,256]{1,0:T(8,128)}, u32[]{:S(2)}) %copy-start.3) | copy-done | bytes 262168
  55.1 0.0 copy-start.4
  55.1 0.9 %copy-done.4 = f32[256,256]{1,0:T(8,128)S(1)} copy-done((f32[256,256]{1,0:T(8,128)S(1)}, f32[256,256]{1,0:T(8,128)}, u32[]{:S(2)}) %copy-start.4) | copy-done | bytes 262168
  56.0 5.0 %update.1 = (f32[256,256]{1,0:T(8,128)}, f32[256,512]{1,0:T(8,128)}, f32[2048,512]{1,0:T(8,128)}) custom-call(f32[256,256]{1,0:T(8,128)S(1)} %copy-done.3, f32[256,256]{1,0:T(8,128)S(1)} %copy-done.4, f32[256,512]{1,0:T(8,128)S(1)} %copy-done.2, f32[2048,256]{1,0:T(8,128)S(1)} %bitcast.1, f32[2048,512]{1,0:T(8,128)S(1)} %copy-done), custom_call_target="tpu_custom_call" | custom-call | tf_op jit(solution)/shard_map/update/pallas_call | solution.py:380
Async XLA Ops:
  49.3 2.2 %copy-start = (f32[2048,512]{1,0:T(8,128)S(1)}, f32[2048,512]{1,0:T(8,128)}, u32[]{:S(2)}) copy-start(f32[2048,512]{1,0:T(8,128)} %trailing_ref.3) | copy-start | bytes 12582916
  51.5 1.6 %copy-start.1 = (f32[4,512,256]{2,1,0:T(8,128)S(1)}, f32[4,512,256]{2,1,0:T(8,128)}, u32[]{:S(2)}) copy-start(f32[4,512,256]{2,1,0:T(8,128)} %get-tuple-element.10) | copy-start | bytes 6291460
  53.1 1.0 %copy-start.2 = (f32[256,512]{1,0:T(8,128)S(1)}, f32[256,512]{1,0:T(8,128)}, u32[]{:S(2)}) copy-start(f32[256,512]{1,0:T(8,128)} %get-tuple-element.9.cross_ref) | copy-start | bytes 1572868
  54.1 0.9 %copy-start.3 = (f32[256,256]{1,0:T(8,128)S(1)}, f32[256,256]{1,0:T(8,128)}, u32[]{:S(2)}) copy-start(f32[256,256]{1,0:T(8,128)} %get-tuple-element.7.r_ref) | copy-start | bytes 786436
  55.1 0.9 %copy-start.4 = (f32[256,256]{1,0:T(8,128)S(1)}, f32[256,256]{1,0:T(8,128)}, u32[]{:S(2)}) copy-start(f32[256,256]{1,0:T(8,128)} %get-tuple-element.8.y_ref) | copy-start | bytes 786436

commit v3 on v2

--- a/solution.py
+++ b/solution.py
@@ -389,7 +389,7 @@
             in_specs=[whole(n, n), whole(n, n), whole(n, width), tall(n), tall(width)],
             out_specs=(whole(n, n), whole(n, width), tall(width)),
             scratch_shapes=[pltpu.VMEM((n, width), jnp.bfloat16)] * 2,
-            compiler_params=pltpu.CompilerParams(vmem_limit_bytes=32 << 20),
+            compiler_params=pltpu.CompilerParams(vmem_limit_bytes=67043328),
         )(r, y, cross, block, trailing)
 
     placed = (P(("rows", "cols"), None), P("rows", "cols"))

time: 61.3 us -> 57.4 us (0.936)
  local copies, waits for them, and re-layouts: 6.71 us -> 0 us
  Pallas kernels: 53.6 us -> 56.6 us
    unnamed x10 -> x0, local copies, waits for them, and re-layouts: 6.71 us -> none
    pallas_call x1, Pallas kernels: 4.97 us -> 7.86 us  [shards(): pl.pallas_call(update, name='update', grid=(height // tile,), out_shape=(...]
where the time goes in v3:
time: 57.4 us; the launch traced here: 57.2 us
  Pallas kernels  56.6 us (99%)
  between operations  0.64 us (1%)
    pallas_call x1, Pallas kernels, shards(): pl.pallas_call(functools.partial(gather_and_factor, nrows, ncols), name='...  48.7 us
    pallas_call x1, Pallas kernels, shards(): pl.pallas_call(update, name='update', grid=(height // tile,), out_shape=(...  7.86 us

profile of v3, /device:TPU:0, one launch (start us, length us, event | category | flops | bytes accessed | tf_op | source)
XLA Modules:
  0.0 57.2 jit_solution(13138192999048954148)
XLA Ops:
  0.6 48.7 %gather_and_factor.1 = (f32[256,256]{1,0:T(8,128)}, f32[256,256]{1,0:T(8,128)}, f32[256,512]{1,0:T(8,128)}, f32[4,512,256]{2,1,0:T(8,128)}) custom-call(f32[512,256]{1,0:T(8,128)} %panel_ref.1, f32[2048,512]{1,0:T(8,128)} %trailing_ref.3), custom_call_target="tpu_custom_call" | custom-call | tf_op jit(solution)/shard_map/gather_and_factor/pallas_call | solution.py:340
  49.4 7.9 %update.1 = (f32[256,256]{1,0:T(8,128)}, f32[256,512]{1,0:T(8,128)}, f32[2048,512]{1,0:T(8,128)}) custom-call(f32[256,256]{1,0:T(8,128)} %get-tuple-element.7.r_ref, f32[256,256]{1,0:T(8,128)} %get-tuple-element.8.y_ref, f32[256,512]{1,0:T(8,128)} %get-tuple-element.9.cross_ref, f32[2048,256]{1,0:T(8,128)} %bitcast.1, f32[2048,512]{1,0:T(8,128)} %trailing_ref.3), custom_call_target="tpu_custom_call" | custom-call | tf_op jit(solution)/shard_map/update/pallas_call | solution.py:380

commit v4 on v3

--- a/solution.py
+++ b/solution.py
@@ -374,7 +374,7 @@
             compiler_params=pltpu.CompilerParams(has_side_effects=True, vmem_limit_bytes=67043328),
         )(panel, trailing)
         block = block.reshape(height, n)
-        tile = min(height, 512)
+        tile = min(height, 256)
         whole = lambda *shape: pl.BlockSpec(shape, lambda i: (0, 0))
         tall = lambda wide: pl.BlockSpec((tile, wide), lambda i: (i, 0))
         return pl.pallas_call(

time: 57.4 us -> 59.4 us (1.035)
  Pallas kernels: 56.6 us -> 58.4 us
    pallas_call x1, Pallas kernels: 7.86 us -> 9.7 us  [shards(): pl.pallas_call(update, name='update', grid=(height // tile,), out_shape=(...]
where the time goes in v4:
time: 59.4 us; the launch traced here: 59.1 us
  Pallas kernels  58.4 us (98%)
  between operations  0.64 us (1%)
    pallas_call x1, Pallas kernels, shards(): pl.pallas_call(functools.partial(gather_and_factor, nrows, ncols), name='...  48.7 us
    pallas_call x1, Pallas kernels, shards(): pl.pallas_call(update, name='update', grid=(height // tile,), out_shape=(...  9.7 us

profile of v4, /device:TPU:0, one launch (start us, length us, event | category | flops | bytes accessed | tf_op | source)
XLA Modules:
  0.0 59.1 jit_solution(15648988687848754930)
XLA Ops:
  0.6 48.7 %gather_and_factor.1 = (f32[256,256]{1,0:T(8,128)}, f32[256,256]{1,0:T(8,128)}, f32[256,512]{1,0:T(8,128)}, f32[4,512,256]{2,1,0:T(8,128)}) custom-call(f32[512,256]{1,0:T(8,128)} %panel_ref.1, f32[2048,512]{1,0:T(8,128)} %trailing_ref.3), custom_call_target="tpu_custom_call" | custom-call | tf_op jit(solution)/shard_map/gather_and_factor/pallas_call | solution.py:340
  49.4 9.7 %update.1 = (f32[256,256]{1,0:T(8,128)}, f32[256,512]{1,0:T(8,128)}, f32[2048,512]{1,0:T(8,128)}) custom-call(f32[256,256]{1,0:T(8,128)} %get-tuple-element.7.r_ref, f32[256,256]{1,0:T(8,128)} %get-tuple-element.8.y_ref, f32[256,512]{1,0:T(8,128)} %get-tuple-element.9.cross_ref, f32[2048,256]{1,0:T(8,128)} %bitcast.1, f32[2048,512]{1,0:T(8,128)} %trailing_ref.3), custom_call_target="tpu_custom_call" | custom-call | tf_op jit(solution)/shard_map/update/pallas_call | solution.py:380
